TPU v7x, 128 devices: a whole 4x4x4 slice. The times are simulated.
128 devices in a mesh: dp: 64 (over y, x, z), rep: 2 (over core).
Axes of the slice: x: 4, y: 4, z: 4, core: 2. Of those that a mesh axis runs over, the one named last changes fastest.
Arguments:
- row_grads: float32 [65536, 512], P(('dp', 'rep')), may hold values from -2500 to 2500
- token_owner: int32 [65536, 1], P(('dp', 'rep')), may hold values from 0 to 63; in each aligned block of 512 rows (0 to 511, 512 to 1023, ...) at most 16 rows name the same one
- token_row: int32 [65536], P(('dp', 'rep')), may hold values from 0 to 2047
- table: float32 [131072, 512], P('dp'), may hold values from -6 to 6
- moment: float32 [131072, 512], P('dp'), may hold values from -3 to 3
- second: float32 [131072, 512], P('dp'), may hold values from 0.05 to 2
Outputs:
- new_table: float32 [131072, 512], P('dp')
- new_moment: float32 [131072, 512], P('dp')
- new_second: float32 [131072, 512], P('dp')
Inputs may be any that keep to these rules, and one draw needn't show every extreme that they name: `token_owner`: among the rows of one device at most 16 name one owner; in every draw some owner is named by exactly 16 rows of some device.
All inputs are finite; a program needn't handle non-finite values.
Results may differ from a plain program's by a relative error of at most 0.00007.
Values sent between devices are 32-bit elements; how exact they have to be, the bound alone decides.
A program may use at most 128 MiB of HBM per device.

v0:
```python
import jax
import jax.numpy as jnp
from jax import lax
from jax.sharding import PartitionSpec as P

VOCAB = 131072
ADAM_STEP = 100
LW = 512


def copy_for_each(value, axis):
    size = lax.axis_size(axis)
    return lax.all_to_all(
        jnp.broadcast_to(value[None], (size, *value.shape)), axis, 0, 0, tiled=True
    )


def of_everyone(value, axis):
    return copy_for_each(value, axis).sum(axis=0)


def accumulate(row_ids, sent_rows, row_start, row_count):
    local_ids = row_ids - row_start
    feature_cols = sent_rows.shape[1]
    inside = (local_ids >= 0) & (local_ids < row_count)
    slot_index = jnp.where(inside, local_ids, row_count)
    return (
        jnp.zeros((row_count, feature_cols), jnp.float32).at[slot_index].add(sent_rows, mode="drop")
    )


def adamw(table_rows, moment_rows, second_rows, dense_grad, scaling):
    clipped = scaling * dense_grad
    new_moment = 0.9 * moment_rows + 0.1 * clipped
    new_second = 0.999 * second_rows + 0.001 * clipped * clipped
    first_fix = 1.0 - 0.9**ADAM_STEP
    second_fix = 1.0 - 0.999**ADAM_STEP
    update = new_moment / first_fix / (jnp.sqrt(new_second / second_fix) + 1e-08)
    new_table = table_rows - 0.01 * (update + 0.01 * table_rows)
    return (new_table, new_moment, new_second)


def clip_factor(total):
    limit = 0.5 * jnp.sqrt(jnp.float32(VOCAB * LW))
    return jnp.minimum(jnp.float32(1.0), limit / (jnp.sqrt(total) + 1e-06))


def local(row_grads, token_owner, token_row, table, moment, second):
    owners = lax.axis_size("dp")
    tokens_here = row_grads.shape[0]
    feature_cols = row_grads.shape[1]
    rows_owned = table.shape[0]
    capacity = 2 * tokens_here // owners
    owner_ids = token_owner[:, 0]
    owner_hits = (owner_ids[:, None] == jnp.arange(owners, dtype=jnp.int32)[None, :]).astype(
        jnp.int32
    )
    earlier = jnp.cumsum(owner_hits, axis=0) - owner_hits
    position = jnp.sum(earlier * owner_hits, axis=1)
    destination = owner_ids * capacity + position
    send_rows = (
        jnp.zeros((owners * capacity, feature_cols), jnp.float32).at[destination].set(row_grads)
    )
    send_ids = jnp.zeros((owners * capacity,), jnp.int32).at[destination].set(token_row)
    received, received_ids = (
        lax.all_to_all(
            send_rows.reshape(owners, capacity, feature_cols),
            "dp",
            split_axis=0,
            concat_axis=0,
            tiled=True,
        ),
        lax.all_to_all(
            send_ids.reshape(owners, capacity), "dp", split_axis=0, concat_axis=0, tiled=True
        ),
    )
    flat_rows = received.reshape(owners * capacity, feature_cols)
    flat_ids = received_ids.reshape(owners * capacity)
    dense = of_everyone(accumulate(flat_ids, flat_rows, 0, rows_owned), "rep")
    total = of_everyone(jnp.sum(dense * dense), "dp")
    scaling = clip_factor(total)
    new_table, new_moment, new_second = adamw(table, moment, second, dense, scaling)
    return (new_table, new_moment, new_second)


def solution(mesh):
    return jax.shard_map(
        local,
        mesh=mesh,
        in_specs=(
            P(("dp", "rep"), None),
            P(("dp", "rep"), None),
            P(("dp", "rep")),
            P("dp", None),
            P("dp", None),
            P("dp", None),
        ),
        out_specs=(P("dp", None), P("dp", None), P("dp", None)),
        check_vma=False,
    )
```

profile of v0, /device:TPU:1, one launch (start us, length us, event | category | flops | bytes accessed | tf_op | source)
XLA Modules:
  0.0 125.0 jit_solution(15020301319457739451)
XLA Ops:
  0.6 0.7 fusion.8
  1.3 1.2 reduce-window.6
  2.5 0.2 slice_reduce_fusion
  2.8 0.8 fusion.7
  3.6 0.7 compare_select_fusion.1
  4.3 2.6 %scatter_custom_fusion = s32[1024]{0:T(1024)S(1)} fusion(s32[512]{0:T(512)S(1)} %bitcast.34, s32[512]{0:T(512)} %param.8, s32[]{:T(128)} %constant.19.clone.1), kind=kCustom, calls=%fused_computation.24 | custom fusion | bytes 4608 | tf_op jit(solution)/shard_map/scatter | solution.py:64
  6.9 0.7 all_to_all.16
  7.6 12.0 %all-to-all-start = ((s32[64,1,16]{2,1,0:T(1,128)}), s32[64,1,16]{2,1,0:T(1,128)S(1)}, u32[]{:S(2)}, u32[]{:S(2)}) async-start(s32[64,1,16]{2,1,0:T(1,128)} %bitcast.5), calls=%async_computation | async-start | bytes 65536 | tf_op jit(solution)/shard_map/all_to_all | solution.py:73
  19.6 4.3 %scatter_custom_fusion.1 = f32[1024,512]{1,0:T(8,128)} fusion(s32[512]{0:T(512)S(1)} %bitcast.35, f32[512,512]{1,0:T(8,128)} %param.6, f32[]{:T(128)} %constant.18.clone.1), kind=kCustom, calls=%fused_computation.10 | custom fusion | bytes 2097664 | tf_op jit(solution)/shard_map/scatter | solution.py:62
  23.9 4.0 %all-to-all-done = s32[64,1,16]{2,1,0:T(1,128)S(1)} async-done(((s32[64,1,16]{2,1,0:T(1,128)}), s32[64,1,16]{2,1,0:T(1,128)S(1)}, u32[]{:S(2)}, u32[]{:S(2)}) %all-to-all-start) | async-done | bytes 4128 | tf_op jit(solution)/shard_map/all_to_all | solution.py:73
  27.9 5.7 %all-to-all-start.1 = ((f32[64,16,512]{2,1,0:T(8,128)}), f32[64,16,512]{2,1,0:T(8,128)S(1)}, u32[]{:S(2)}, u32[]{:S(2)}) async-start(f32[64,16,512]{2,1,0:T(8,128)} %bitcast.7), calls=%async_computation.1 | async-start | bytes 4194304 | tf_op jit(solution)/shard_map/all_to_all | solution.py:66
  33.7 0.5 broadcast.95
  34.2 0.7 reduce.6
  34.9 0.1 reshape.82
  35.0 25.9 %all-to-all-done.1 = f32[64,16,512]{2,1,0:T(8,128)S(1)} async-done(((f32[64,16,512]{2,1,0:T(8,128)}), f32[64,16,512]{2,1,0:T(8,128)S(1)}, u32[]{:S(2)}, u32[]{:S(2)}) %all-to-all-start.1) | async-done | bytes 2097184 | tf_op jit(solution)/shard_map/all_to_all | solution.py:66
  60.9 8.8 %scatter_custom_fusion.2 = f32[2048,512]{1,0:T(8,128)} fusion(s32[1024]{0:T(1024)S(1)} %bitcast.33, f32[1024,512]{1,0:T(8,128)S(1)} %bitcast.29, f32[]{:T(128)} %constant.18.clone.1), kind=kCustom, calls=%fused_computation.8 | custom fusion | flops 524288 | bytes 4194308 | tf_op jit(solution)/shard_map/scatter-add | solution.py:28
  69.7 3.4 %broadcast_in_dim.12 = f32[2,2048,512]{2,1,0:T(8,128)S(1)} broadcast(f32[2048,512]{1,0:T(8,128)} %scatter_custom_fusion.2), dimensions={1,2} | broadcast | bytes 12582912 | tf_op jit(solution)/shard_map/broadcast_in_dim | solution.py:14
  73.1 14.8 %all_to_all.25 = f32[2,2048,512]{2,1,0:T(8,128)} all-to-all(f32[2,2048,512]{2,1,0:T(8,128)S(1)} %broadcast_in_dim.12), channel_id=1, replica_groups=mesh['dp'=64,'rep'=2] {'rep'}, dimensions={0} | all-to-all | bytes 16777216 | tf_op jit(solution)/shard_map/all_to_all | solution.py:13
  87.9 6.8 %reduce_sum.40 = f32[2048,512]{1,0:T(8,128)} reduce(f32[2,2048,512]{2,1,0:T(8,128)} %all_to_all.25, f32[]{:T(128)} %constant.18.clone.1), dimensions={0}, to_apply=%region_6.7 | reduce | flops 1048576 | bytes 12582916 | tf_op jit(solution)/shard_map/reduce_sum | solution.py:19
  94.7 3.9 %multiply_reduce_fusion = f32[]{:T(128)} fusion(f32[2048,512]{1,0:T(8,128)} %reduce_sum.40), kind=kLoop, calls=%fused_computation.7 | loop fusion | flops 2097151 | bytes 4194308 | tf_op jit(solution)/shard_map/reduce_sum | solution.py:80
  98.6 0.7 broadcast_in_dim.13
  99.3 13.2 %all_to_all.26 = f32[64,1,1]{2,1,0:T(1,128)S(1)} all-to-all(f32[64,1,1]{2,1,0:T(1,128)S(1)} %broadcast_in_dim.13), channel_id=1, replica_groups=mesh['dp'=64,'rep'=2] {'dp'}, dimensions={0} | all-to-all | bytes 512 | tf_op jit(solution)/shard_map/all_to_all | solution.py:13
  112.4 0.7 reduce_sum.42
  113.8 11.2 %multiply_subtract_fusion = (f32[2048,512]{1,0:T(8,128)}, f32[2048,512]{1,0:T(8,128)}, f32[2048,512]{1,0:T(8,128)}) fusion(f32[2048,512]{1,0:T(8,128)} %param.9, f32[2048,512]{1,0:T(8,128)} %reduce_sum.40, f32[]{:T(128)S(6)} %min_shard_map.3, f32[2048,512]{1,0:T(8,128)} %param.10, f32[2048,512]{1,0:T(8,128)} %param.11), kind=kLoop, calls=%fused_computation.5 | loop fusion | flops 16777216 | bytes 29360132 | tf_op jit(solution)/shard_map/sub | solution.py:39
  (3 shorter events, 0.1 us)
Async XLA Ops:
  7.6 20.3 %all-to-all-start = ((s32[64,1,16]{2,1,0:T(1,128)}), s32[64,1,16]{2,1,0:T(1,128)S(1)}, u32[]{:S(2)}, u32[]{:S(2)}) async-start(s32[64,1,16]{2,1,0:T(1,128)} %bitcast.5), calls=%async_computation | async-start | bytes 65536 | tf_op jit(solution)/shard_map/all_to_all | solution.py:73
  27.9 33.0 %all-to-all-start.1 = ((f32[64,16,512]{2,1,0:T(8,128)}), f32[64,16,512]{2,1,0:T(8,128)S(1)}, u32[]{:S(2)}, u32[]{:S(2)}) async-start(f32[64,16,512]{2,1,0:T(8,128)} %bitcast.7), calls=%async_computation.1 | async-start | bytes 4194304 | tf_op jit(solution)/shard_map/all_to_all | solution.py:66
where the time goes:
time: 126 us; the launch traced here: 125 us
  other arithmetic  35.5 us (28%)
  waiting for transfers between devices  29.9 us (24%)
  blocking collectives  28 us (22%)
  starting transfers between devices  17.7 us (14%)
  local copies, waits for them, and re-layouts  12.5 us (10%)
  between operations  1.43 us (1%)
    all_to_all x2, blocking collectives, copy_for_each(): lax.all_to_all(jnp.broadcast_to(value[None], (size, *value.shape)), axis,...  28 us
    all_to_all x1, waiting for transfers between devices, local(): lax.all_to_all(send_rows.reshape(owners, capacity, feature_cols), 'dp', s...  25.9 us
    all_to_all x1, starting transfers between devices, local(): lax.all_to_all(send_ids.reshape(owners, capacity), 'dp', split_axis=0, co...  12 us
    sub x1, other arithmetic, adamw(): new_table = table_rows - 0.01 * (update + 0.01 * table_rows)  11.2 us
    scatter-add x1, other arithmetic, accumulate(): jnp.zeros((row_count, feature_cols), jnp.float32).at[slot_index]  8.81 us
    reduce_sum x2, other arithmetic, of_everyone(): return copy_for_each(value, axis).sum(axis=0)  7.48 us
    all_to_all x1, starting transfers between devices, local(): lax.all_to_all(send_rows.reshape(owners, capacity, feature_cols), 'dp', s...  5.75 us
    scatter x1, local copies, waits for them, and re-layouts, local(): jnp.zeros((owners * capacity, feature_cols), jnp.float32).at[destination]  4.32 us
  transfers between devices with their start and end apart: 2, of which 2 were waited for; matrix products, arithmetic and copies ran while one was open for 5% of the time, Pallas kernels for 0%

commit v1 on v0

v1 whole, which is shorter than its diff:
```python
import functools

import jax
import jax.numpy as jnp
from jax import lax
from jax.experimental import pallas as pl
from jax.experimental.pallas import tpu as pltpu
from jax.sharding import PartitionSpec as P

VOCAB = 131072
ADAM_STEP = 100
LW = 512
OWNERS = 64
CAP = 16
ROWS = 2048
TOK = 512
HALF = 256
STEP = 27
MESH = pl.DeviceIdType.MESH
F32 = jnp.float32
BF16 = jnp.bfloat16


def two_parts(value):
    high = value.astype(BF16)
    return high, (value - high.astype(F32)).astype(BF16)


def iota(shape, axis):
    return lax.broadcasted_iota(jnp.int32, shape, axis)


def onehot(mask):
    return jnp.where(mask, 1.0, 0.0).astype(BF16)


def exchange_kernel(
    owner_hbm, row_hbm, grads_hbm, table_hbm, moment_hbm, second_hbm,
    dense, table_out, moment_out, second_out, clip_out,
    owner_ref, row_ref, grads, send, recv, ids_send, ids_recv, ids_own, ids_other, part, parts,
    load_sem, state_sem, ids_sem, ids_got, swap_sem, swap_got,
    send_sem, recv_sem, part_sem, part_got, half_sem, half_got,
):
    me = lax.axis_index("dp")
    core = lax.axis_index("rep")
    y, x, z = me // 16, (me // 4) % 4, me % 4

    def ahead(offset):
        oy, ox, oz = offset // 16, (offset // 4) % 4, offset % 4
        return ((y + oy) % 4) * 16 + ((x + ox) % 4) * 4 + (z + oz) % 4

    loads = [
        pltpu.make_async_copy(source, target, load_sem.at[k])
        for k, (source, target) in enumerate(
            ((owner_hbm, owner_ref), (row_hbm, row_ref), (grads_hbm, grads))
        )
    ]
    for load in loads:
        load.start()
    barrier = pltpu.get_barrier_semaphore()
    for offset in range(1, OWNERS):
        for flip in range(2):
            pl.semaphore_signal(
                barrier, inc=1, device_id=(ahead(offset), (core + flip) % 2), device_id_type=MESH
            )
    pl.semaphore_signal(barrier, inc=1, device_id=(me, 1 - core), device_id_type=MESH)
    states = [
        pltpu.make_async_copy(source, target, state_sem.at[k])
        for k, (source, target) in enumerate(
            ((table_hbm, table_out), (moment_hbm, moment_out), (second_hbm, second_out))
        )
    ]
    for state in states:
        state.start()

    loads[0].wait()
    loads[1].wait()
    owner = owner_ref[...]
    hits = iota((OWNERS, TOK), 0) == owner
    before = onehot(iota((TOK, TOK), 0) < iota((TOK, TOK), 1))
    earlier = jnp.dot(onehot(hits), before, preferred_element_type=F32)
    rank = jnp.sum(jnp.where(hits, earlier, 0.0), axis=0, keepdims=True)
    slot = owner.astype(F32) * float(CAP) + rank

    row = row_ref[...]
    row_high = (row // 64).astype(F32)
    row_low = (row % 64).astype(F32)
    spread = onehot((iota((128, TOK), 0) % CAP).astype(F32) == rank)
    contract = (((1,), (1,)), ((), ()))
    ids = 64.0 * lax.dot_general(
        jnp.where(hits, row_high, 0.0).astype(BF16), spread, contract, preferred_element_type=F32
    ) + lax.dot_general(
        jnp.where(hits, row_low, 0.0).astype(BF16), spread, contract, preferred_element_type=F32
    )
    ids_send[...] = ids.reshape(OWNERS, 1, 128)

    loads[2].wait()
    grads_parts = jnp.concatenate(two_parts(grads[...]), axis=0)

    def place(block, carry):
        pick = onehot((iota((256, TOK), 0) + block * 256).astype(F32) == slot)
        rows = jnp.dot(
            jnp.concatenate((pick, pick), axis=1), grads_parts, preferred_element_type=F32
        )
        send[pl.ds(block * 16, 16), 0] = rows[:, :HALF].reshape(16, CAP, HALF)
        send[pl.ds(block * 16, 16), 1] = rows[:, HALF:].reshape(16, CAP, HALF)
        return carry

    lax.fori_loop(0, 4, place, 0)

    def clear(block, carry):
        dense[core, pl.ds(block * 256, 256)] = jnp.zeros((256, HALF), F32)
        return carry

    lax.fori_loop(0, ROWS // 256, clear, 0)
    recv[119] = send[me, core]
    ids_recv[63] = ids_send[me]

    pl.semaphore_wait(barrier, 127)

    def send_ids(j, carry):
        target = ahead(((j + 1) * STEP) % OWNERS)
        pltpu.make_async_remote_copy(
            ids_send.at[target], ids_recv.at[j], ids_sem, ids_got,
            device_id=(target, core), device_id_type=MESH,
        ).start()
        return carry

    lax.fori_loop(0, 63, send_ids, 0)

    def send_rows(j, carry):
        target = ahead(((j + 1) * STEP) % OWNERS)
        place_at = (j // 8) * 16 + j % 8
        for flip in range(2):
            half = (core + flip) % 2
            pltpu.make_async_remote_copy(
                send.at[target, half], recv.at[place_at + 8 * flip], send_sem,
                recv_sem.at[j // 8], device_id=(target, half), device_id_type=MESH,
            ).start()
        return carry

    lax.fori_loop(0, 63, send_rows, 0)
    pltpu.make_async_remote_copy(
        send.at[me, 1 - core], recv.at[127], send_sem, recv_sem.at[7],
        device_id=(me, 1 - core), device_id_type=MESH,
    ).start()

    pltpu.make_async_copy(ids_recv.at[pl.ds(0, 63)], ids_recv.at[pl.ds(0, 63)], ids_got).wait()
    got = ids_recv[...].reshape(8, 8, 128)
    keep = iota((8, 8, 128), 2) // CAP == iota((8, 8, 128), 1)
    ids_own[...] = jnp.sum(jnp.where(keep, got, 0.0), axis=1)
    swap = pltpu.make_async_remote_copy(
        ids_own, ids_other, swap_sem, swap_got, device_id=(me, 1 - core), device_id_type=MESH
    )
    swap.start()
    swap.wait_recv()

    def gather(group):
        near = ids_own[pl.ds(group, 1), :]
        far = ids_other[pl.ds(group, 1), :]
        ids_here = jnp.concatenate((near, far), axis=1)
        values = jnp.concatenate(
            two_parts(recv[pl.ds(group * 16, 16)].reshape(256, HALF)), axis=0
        )

        def rows_block(block, carry):
            pick = onehot((iota((512, 256), 0) + block * 512).astype(F32) == ids_here)
            dense[core, pl.ds(block * 512, 512)] += jnp.dot(
                jnp.concatenate((pick, pick), axis=1), values, preferred_element_type=F32
            )
            return carry

        lax.fori_loop(0, ROWS // 512, rows_block, 0)

    def group_step(group, carry):
        here = recv.at[pl.ds(group * 16, 16)]
        pltpu.make_async_copy(here, here, recv_sem.at[group]).wait()
        gather(group)
        return carry

    lax.fori_loop(0, 7, group_step, 0)
    last = recv.at[pl.ds(112, 15)]
    pltpu.make_async_copy(last, last, recv_sem.at[7]).wait()
    gather(7)

    def square(block, carry):
        value = dense[core, pl.ds(block * 64, 64)]
        return carry + jnp.sum((value * value).reshape(8, 8, HALF), axis=0)

    squares = lax.fori_loop(0, ROWS // 64, square, jnp.zeros((8, HALF), F32))
    squares = jnp.sum(squares[:, :128] + squares[:, 128:], axis=0, keepdims=True)
    part[...] = squares
    parts[core] = squares
    half_copy = pltpu.make_async_remote_copy(
        dense.at[core], dense.at[core], half_sem, half_got,
        device_id=(me, 1 - core), device_id_type=MESH,
    )
    for offset in [42, *(o for o in range(1, OWNERS) if o != 42)]:
        for flip in range(2):
            pltpu.make_async_remote_copy(
                part, parts.at[2 * offset + core], part_sem, part_got,
                device_id=(ahead(offset), (core + flip) % 2), device_id_type=MESH,
            ).start()
    pltpu.make_async_remote_copy(
        part, parts.at[core], part_sem, part_got,
        device_id=(me, 1 - core), device_id_type=MESH,
    ).start()
    half_copy.start()
    for state in states:
        state.wait()
    swap.wait_send()
    pltpu.make_async_copy(ids_send.at[pl.ds(0, 63)], ids_send.at[pl.ds(0, 63)], ids_sem).wait()
    sent = recv.at[pl.ds(0, 127)]
    pltpu.make_async_copy(sent, sent, send_sem).wait()
    row_count = parts.at[pl.ds(0, 127)]
    pltpu.make_async_copy(row_count, row_count, part_got).wait()
    total = jnp.sum(jnp.sum(parts[...], axis=0), axis=1, keepdims=True)
    limit = 0.5 * jnp.sqrt(jnp.float32(VOCAB * LW))
    scaling = jnp.minimum(1.0, limit / (jnp.sqrt(total) + 1e-06))
    clip_out[...] = jnp.broadcast_to(scaling, (8, 128))
    half_copy.wait()
    pltpu.make_async_copy(row_count, row_count, part_sem).wait()


def exchange(row_grads, token_owner, token_row, table, moment, second):
    vmem = pl.BlockSpec(memory_space=pltpu.VMEM)
    hbm = pl.BlockSpec(memory_space=pl.ANY)
    dma = pltpu.SemaphoreType.DMA
    state = pltpu.VMEM((ROWS, LW), F32)
    return pl.pallas_call(
        exchange_kernel,
        out_shape=(pltpu.VMEM((2, ROWS, HALF), F32), state, state, state, pltpu.VMEM((8, 128), F32)),
        in_specs=[hbm] * 6,
        out_specs=(vmem,) * 5,
        scratch_shapes=[
            pltpu.VMEM((1, TOK), jnp.int32),
            pltpu.VMEM((1, TOK), jnp.int32),
            pltpu.VMEM((TOK, LW), F32),
            pltpu.VMEM((OWNERS, 2, CAP, HALF), F32),
            pltpu.VMEM((128, CAP, HALF), F32),
            pltpu.VMEM((OWNERS, 1, 128), F32),
            pltpu.VMEM((OWNERS, 1, 128), F32),
            pltpu.VMEM((8, 128), F32),
            pltpu.VMEM((8, 128), F32),
            pltpu.VMEM((1, 128), F32),
            pltpu.VMEM((128, 1, 128), F32),
            dma((3,)), dma((3,)), dma, dma, dma, dma, dma, dma((8,)), dma, dma, dma, dma,
        ],
        compiler_params=pltpu.CompilerParams(
            collective_id=0, has_side_effects=True, vmem_limit_bytes=24 * 2**20
        ),
        name="exchange",
    )(
        *(
            pltpu.with_memory_space_constraint(value, pltpu.HBM)
            for value in (
                token_owner.reshape(1, TOK),
                token_row.reshape(1, TOK),
                row_grads,
                table,
                moment,
                second,
            )
        ),
    )


BLOCK = 128
PIECE = 32


def update_kernel(
    dense, table, moment, second, clip,
    table_hbm, moment_hbm, second_hbm,
    table_out, moment_out, second_out, sems,
):
    scaling = jnp.concatenate((clip[...], clip[...]), axis=1)[:1]
    first_fix = 1.0 / (1.0 - 0.9**ADAM_STEP)
    second_fix = 1.0 / (1.0 - 0.999**ADAM_STEP)
    pairs = (
        (table_out, table_hbm),
        (moment_out, moment_hbm),
        (second_out, second_hbm),
    )

    def block_step(block, carry):
        def piece_step(piece, inner):
            rows = pl.ds(pl.multiple_of(block * BLOCK + piece * PIECE, PIECE), PIECE)
            for half in range(2):
                cols = pl.ds(half * HALF, HALF)
                grad = scaling * dense[half, rows, :]
                new_moment = 0.9 * moment[rows, cols] + 0.1 * grad
                new_second = 0.999 * second[rows, cols] + 0.001 * grad * grad
                update = (new_moment * first_fix) / (jnp.sqrt(new_second * second_fix) + 1e-08)
                old = table[rows, cols]
                table_out[rows, cols] = old - 0.01 * (update + 0.01 * old)
                moment_out[rows, cols] = new_moment
                second_out[rows, cols] = new_second
            return inner

        lax.fori_loop(0, BLOCK // PIECE, piece_step, 0)
        span = pl.ds(pl.multiple_of(block * BLOCK, BLOCK), BLOCK)
        for k, (source, target) in enumerate(pairs):
            pltpu.make_async_copy(source.at[span], target.at[span], sems.at[k]).start()
        return carry

    lax.fori_loop(0, ROWS // BLOCK, block_step, 0)
    for k, (source, target) in enumerate(pairs):
        pltpu.make_async_copy(source, target, sems.at[k]).wait()


def update(dense, table, moment, second, clip):
    vmem = pl.BlockSpec(memory_space=pltpu.VMEM)
    hbm = pl.BlockSpec(memory_space=pl.ANY)
    out = jax.ShapeDtypeStruct((ROWS, LW), F32)
    args = [
        pltpu.with_memory_space_constraint(value, pltpu.VMEM)
        for value in (dense, table, moment, second, clip)
    ]
    return pl.pallas_call(
        update_kernel,
        out_shape=(out, out, out),
        in_specs=[vmem] * 5,
        out_specs=(hbm,) * 3,
        scratch_shapes=[pltpu.VMEM((ROWS, LW), F32)] * 3 + [pltpu.SemaphoreType.DMA((3,))],
        compiler_params=pltpu.CompilerParams(vmem_limit_bytes=32 * 2**20),
        name="update",
    )(*args)


def local(row_grads, token_owner, token_row, table, moment, second):
    return update(*exchange(row_grads, token_owner, token_row, table, moment, second))


def solution(mesh):
    return jax.shard_map(
        local,
        mesh=mesh,
        in_specs=(
            P(("dp", "rep"), None),
            P(("dp", "rep"), None),
            P(("dp", "rep")),
            P("dp", None),
            P("dp", None),
            P("dp", None),
        ),
        out_specs=(P("dp", None), P("dp", None), P("dp", None)),
        check_vma=False,
    )
```

time: 126 us -> 53.3 us (0.42)
  Pallas kernels: 0 us -> 52.6 us
  other arithmetic: 35.5 us -> 0 us
  waiting for transfers between devices: 29.9 us -> 0 us
  blocking collectives: 28 us -> 0 us
  starting transfers between devices: 17.7 us -> 0 us
  local copies, waits for them, and re-layouts: 12.5 us -> 0 us
    pallas_call x0 -> x2, Pallas kernels: none -> 52.6 us  [the longest x1 47.4 us: exchange(): pl.pallas_call(exchange_kernel, out_shape=(pltpu.VMEM((2, ROWS, HALF), F3...]
    all_to_all x2 -> x0, waiting for transfers between devices: 29.9 us -> none  [the longest x1 25.9 us: local(): lax.all_to_all(send_rows.reshape(owners, capacity, feature_cols), 'dp', s...]
    all_to_all x2 -> x0, blocking collectives: 28 us -> none  [copy_for_each(): lax.all_to_all(jnp.broadcast_to(value[None], (size, *value.shape)), axis,...]
    all_to_all x2 -> x0, starting transfers between devices: 17.7 us -> none  [the longest x1 12 us: local(): lax.all_to_all(send_ids.reshape(owners, capacity), 'dp', split_axis=0, co...]
    reduce_sum x4 -> x0, other arithmetic: 12.1 us -> none  [the longest x2 7.48 us: of_everyone(): return copy_for_each(value, axis).sum(axis=0)]
    sub x1 -> x0, other arithmetic: 11.2 us -> none  [adamw(): new_table = table_rows - 0.01 * (update + 0.01 * table_rows)]
    scatter-add x1 -> x0, other arithmetic: 8.81 us -> none  [accumulate(): jnp.zeros((row_count, feature_cols), jnp.float32).at[slot_index]]
    scatter x2 -> x0, local copies, waits for them, and re-layouts: 6.92 us -> none  [the longest x1 4.32 us: local(): jnp.zeros((owners * capacity, feature_cols), jnp.float32).at[destination]]
  transfers between devices with their start and end apart: 2 -> 0, of which waited for: 2 -> 0; matrix products, arithmetic and copies ran while one was open for 5% -> 0% of each run, Pallas kernels for 0% -> 0%
where the time goes in v1:
time: 53.3 us; the launch traced here: 53.2 us
  Pallas kernels  52.6 us (99%)
  between operations  0.64 us (1%)
    pallas_call x1, Pallas kernels, exchange(): pl.pallas_call(exchange_kernel, out_shape=(pltpu.VMEM((2, ROWS, HALF), F3...  47.4 us
    pallas_call x1, Pallas kernels, update(): pl.pallas_call(update_kernel, out_shape=(out, out, out), in_specs=[vmem]...  5.22 us

profile of v1, /device:TPU:1, one launch (start us, length us, event | category | flops | bytes accessed | tf_op | source)
XLA Modules:
  0.0 53.2 jit_solution(17837284524798719712)
XLA Ops:
  0.6 47.4 %exchange.1 = (f32[2,2048,256]{2,1,0:T(8,128)S(1)}, f32[2048,512]{1,0:T(8,128)S(1)}, f32[2048,512]{1,0:T(8,128)S(1)}, f32[2048,512]{1,0:T(8,128)S(1)}, f32[8,128]{1,0:T(8,128)S(1)}) custom-call(s32[1,512]{1,0:T(1,128)} %bitcast.2, s32[1,512]{1,0:T(1,128)} %bitcast.3, f32[512,512]{1,0:T(8,128)} %grads_hbm.1, f32[2048,512]{1,0:T(8,128)} %table_hbm.1, ...), custom_call_target="tpu_custom_call" | custom-call | tf_op jit(solution)/shard_map/exchange/pallas_call | solution.py:230
  48.0 5.2 %update.1 = (f32[2048,512]{1,0:T(8,128)}, f32[2048,512]{1,0:T(8,128)}, f32[2048,512]{1,0:T(8,128)}) custom-call(f32[2,2048,256]{2,1,0:T(8,128)S(1)} %get-tuple-element.8.dense, f32[2048,512]{1,0:T(8,128)S(1)} %get-tuple-element.9.table, f32[2048,512]{1,0:T(8,128)S(1)} %get-tuple-element.10.moment, f32[2048,512]{1,0:T(8,128)S(1)} %get-tuple-element.11.second, ...), custom_call_target="tpu_custom_call" | custom-call | tf_op jit(solution)/shard_map/update/pallas_call | solution.py:320

commit v2 on v1

--- a/solution.py
+++ b/solution.py
@@ -15,10 +15,37 @@
 ROWS = 2048
 TOK = 512
 HALF = 256
-STEP = 27
 MESH = pl.DeviceIdType.MESH
 F32 = jnp.float32
 BF16 = jnp.bfloat16
+
+
+def hops(offset):
+    return [min(step, 4 - step) for step in (offset // 16, (offset // 4) % 4, offset % 4)]
+
+
+def opposite(offset):
+    oy, ox, oz = offset // 16, (offset // 4) % 4, offset % 4
+    return (-oy % 4) * 16 + (-ox % 4) * 4 + -oz % 4
+
+
+def turned(offset):
+    return (offset % 16) * 4 + offset // 16
+
+
+def balanced(offsets):
+    order = []
+    for start in sorted(offsets, key=lambda offset: (-sum(hops(offset)), offset)):
+        offset = start
+        for _ in range(3):
+            for member in (offset, opposite(offset)):
+                if member not in order:
+                    order.append(member)
+            offset = turned(offset)
+    return order
+
+
+FAR_FIRST = balanced(range(1, OWNERS))
 
 
 def two_parts(value):
@@ -58,7 +85,7 @@
     for load in loads:
         load.start()
     barrier = pltpu.get_barrier_semaphore()
-    for offset in range(1, OWNERS):
+    for offset in FAR_FIRST:
         for flip in range(2):
             pl.semaphore_signal(
                 barrier, inc=1, device_id=(ahead(offset), (core + flip) % 2), device_id_type=MESH
@@ -118,28 +145,20 @@
 
     pl.semaphore_wait(barrier, 127)
 
-    def send_ids(j, carry):
-        target = ahead(((j + 1) * STEP) % OWNERS)
+    for j, offset in enumerate(FAR_FIRST):
+        target = ahead(offset)
         pltpu.make_async_remote_copy(
             ids_send.at[target], ids_recv.at[j], ids_sem, ids_got,
             device_id=(target, core), device_id_type=MESH,
         ).start()
-        return carry
-
-    lax.fori_loop(0, 63, send_ids, 0)
-
-    def send_rows(j, carry):
-        target = ahead(((j + 1) * STEP) % OWNERS)
-        place_at = (j // 8) * 16 + j % 8
+    for j, offset in enumerate(FAR_FIRST):
+        target = ahead(offset)
         for flip in range(2):
             half = (core + flip) % 2
             pltpu.make_async_remote_copy(
-                send.at[target, half], recv.at[place_at + 8 * flip], send_sem,
+                send.at[target, half], recv.at[(j // 8) * 16 + j % 8 + 8 * flip], send_sem,
                 recv_sem.at[j // 8], device_id=(target, half), device_id_type=MESH,
             ).start()
-        return carry
-
-    lax.fori_loop(0, 63, send_rows, 0)
     pltpu.make_async_remote_copy(
         send.at[me, 1 - core], recv.at[127], send_sem, recv_sem.at[7],
         device_id=(me, 1 - core), device_id_type=MESH,
@@ -155,7 +174,7 @@
     swap.start()
     swap.wait_recv()
 
-    def gather(group):
+    def gather(group, squares=None):
         near = ids_own[pl.ds(group, 1), :]
         far = ids_other[pl.ds(group, 1), :]
         ids_here = jnp.concatenate((near, far), axis=1)
@@ -164,13 +183,17 @@
         )
 
         def rows_block(block, carry):
-            pick = onehot((iota((512, 256), 0) + block * 512).astype(F32) == ids_here)
-            dense[core, pl.ds(block * 512, 512)] += jnp.dot(
+            pick = onehot((iota((1024, 256), 0) + block * 1024).astype(F32) == ids_here)
+            rows = pl.ds(block * 1024, 1024)
+            total = dense[core, rows] + jnp.dot(
                 jnp.concatenate((pick, pick), axis=1), values, preferred_element_type=F32
             )
-            return carry
-
-        lax.fori_loop(0, ROWS // 512, rows_block, 0)
+            dense[core, rows] = total
+            if squares is None:
+                return carry
+            return carry + jnp.sum((total * total).reshape(128, 8, HALF), axis=0)
+
+        return lax.fori_loop(0, ROWS // 1024, rows_block, 0 if squares is None else squares)
 
     def group_step(group, carry):
         here = recv.at[pl.ds(group * 16, 16)]
@@ -181,13 +204,7 @@
     lax.fori_loop(0, 7, group_step, 0)
     last = recv.at[pl.ds(112, 15)]
     pltpu.make_async_copy(last, last, recv_sem.at[7]).wait()
-    gather(7)
-
-    def square(block, carry):
-        value = dense[core, pl.ds(block * 64, 64)]
-        return carry + jnp.sum((value * value).reshape(8, 8, HALF), axis=0)
-
-    squares = lax.fori_loop(0, ROWS // 64, square, jnp.zeros((8, HALF), F32))
+    squares = gather(7, jnp.zeros((8, HALF), F32))
     squares = jnp.sum(squares[:, :128] + squares[:, 128:], axis=0, keepdims=True)
     part[...] = squares
     parts[core] = squares
@@ -195,7 +212,7 @@
         dense.at[core], dense.at[core], half_sem, half_got,
         device_id=(me, 1 - core), device_id_type=MESH,
     )
-    for offset in [42, *(o for o in range(1, OWNERS) if o != 42)]:
+    for offset in FAR_FIRST:
         for flip in range(2):
             pltpu.make_async_remote_copy(
                 part, parts.at[2 * offset + core], part_sem, part_got,
@@ -266,7 +283,7 @@
 
 
 BLOCK = 128
-PIECE = 32
+PIECE = 64
 
 
 def update_kernel(

time: 53.3 us -> 49.9 us (0.936)
  Pallas kernels: 52.6 us -> 49.2 us
    pallas_call x1, Pallas kernels: 47.4 us -> 44.4 us  [exchange(): pl.pallas_call(exchange_kernel, out_shape=(pltpu.VMEM((2, ROWS, HALF), F3...]
where the time goes in v2:
time: 49.9 us; the launch traced here: 49.8 us
  Pallas kernels  49.2 us (99%)
  between operations  0.64 us (1%)
    pallas_call x1, Pallas kernels, exchange(): pl.pallas_call(exchange_kernel, out_shape=(pltpu.VMEM((2, ROWS, HALF), F3...  44.4 us
    pallas_call x1, Pallas kernels, update(): pl.pallas_call(update_kernel, out_shape=(out, out, out), in_specs=[vmem]...  4.78 us

profile of v2, /device:TPU:1, one launch (start us, length us, event | category | flops | bytes accessed | tf_op | source)
XLA Modules:
  0.0 49.8 jit_solution(9557154153130377948)
XLA Ops:
  0.6 44.4 %exchange.1 = (f32[2,2048,256]{2,1,0:T(8,128)S(1)}, f32[2048,512]{1,0:T(8,128)S(1)}, f32[2048,512]{1,0:T(8,128)S(1)}, f32[2048,512]{1,0:T(8,128)S(1)}, f32[8,128]{1,0:T(8,128)S(1)}) custom-call(s32[1,512]{1,0:T(1,128)} %bitcast.2, s32[1,512]{1,0:T(1,128)} %bitcast.3, f32[512,512]{1,0:T(8,128)} %grads_hbm.1, f32[2048,512]{1,0:T(8,128)} %table_hbm.1, ...), custom_call_target="tpu_custom_call" | custom-call | tf_op jit(solution)/shard_map/exchange/pallas_call | solution.py:247
  45.0 4.8 %update.1 = (f32[2048,512]{1,0:T(8,128)}, f32[2048,512]{1,0:T(8,128)}, f32[2048,512]{1,0:T(8,128)}) custom-call(f32[2,2048,256]{2,1,0:T(8,128)S(1)} %get-tuple-element.8.dense, f32[2048,512]{1,0:T(8,128)S(1)} %get-tuple-element.9.table, f32[2048,512]{1,0:T(8,128)S(1)} %get-tuple-element.10.moment, f32[2048,512]{1,0:T(8,128)S(1)} %get-tuple-element.11.second, ...), custom_call_target="tpu_custom_call" | custom-call | tf_op jit(solution)/shard_map/update/pallas_call | solution.py:337

commit v3 on v2

--- a/solution.py
+++ b/solution.py
@@ -174,7 +174,7 @@
     swap.start()
     swap.wait_recv()
 
-    def gather(group, squares=None):
+    def gather(group):
         near = ids_own[pl.ds(group, 1), :]
         far = ids_other[pl.ds(group, 1), :]
         ids_here = jnp.concatenate((near, far), axis=1)
@@ -182,18 +182,12 @@
             two_parts(recv[pl.ds(group * 16, 16)].reshape(256, HALF)), axis=0
         )
 
-        def rows_block(block, carry):
-            pick = onehot((iota((1024, 256), 0) + block * 1024).astype(F32) == ids_here)
-            rows = pl.ds(block * 1024, 1024)
-            total = dense[core, rows] + jnp.dot(
-                jnp.concatenate((pick, pick), axis=1), values, preferred_element_type=F32
-            )
-            dense[core, rows] = total
-            if squares is None:
-                return carry
-            return carry + jnp.sum((total * total).reshape(128, 8, HALF), axis=0)
-
-        return lax.fori_loop(0, ROWS // 1024, rows_block, 0 if squares is None else squares)
+        pick = onehot(iota((ROWS, 256), 0).astype(F32) == ids_here)
+        total = dense[core] + jnp.dot(
+            jnp.concatenate((pick, pick), axis=1), values, preferred_element_type=F32
+        )
+        dense[core] = total
+        return total
 
     def group_step(group, carry):
         here = recv.at[pl.ds(group * 16, 16)]
@@ -204,7 +198,8 @@
     lax.fori_loop(0, 7, group_step, 0)
     last = recv.at[pl.ds(112, 15)]
     pltpu.make_async_copy(last, last, recv_sem.at[7]).wait()
-    squares = gather(7, jnp.zeros((8, HALF), F32))
+    total = gather(7)
+    squares = jnp.sum((total * total).reshape(ROWS // 8, 8, HALF), axis=0)
     squares = jnp.sum(squares[:, :128] + squares[:, 128:], axis=0, keepdims=True)
     part[...] = squares
     parts[core] = squares

time: 49.9 us -> 49.3 us (0.988)
  Pallas kernels: 49.2 us -> 48.6 us
    pallas_call x1, Pallas kernels: 44.4 us -> 43.8 us  [exchange(): pl.pallas_call(exchange_kernel, out_shape=(pltpu.VMEM((2, ROWS, HALF), F3...]
where the time goes in v3:
time: 49.3 us; the launch traced here: 49.2 us
  Pallas kernels  48.6 us (99%)
  between operations  0.64 us (1%)
    pallas_call x1, Pallas kernels, exchange(): pl.pallas_call(exchange_kernel, out_shape=(pltpu.VMEM((2, ROWS, HALF), F3...  43.8 us
    pallas_call x1, Pallas kernels, update(): pl.pallas_call(update_kernel, out_shape=(out, out, out), in_specs=[vmem]...  4.78 us

profile of v3, /device:TPU:1, one launch (start us, length us, event | category | flops | bytes accessed | tf_op | source)
XLA Modules:
  0.0 49.2 jit_solution(5039771928735152258)
XLA Ops:
  0.6 43.8 %exchange.1 = (f32[2,2048,256]{2,1,0:T(8,128)S(1)}, f32[2048,512]{1,0:T(8,128)S(1)}, f32[2048,512]{1,0:T(8,128)S(1)}, f32[2048,512]{1,0:T(8,128)S(1)}, f32[8,128]{1,0:T(8,128)S(1)}) custom-call(s32[1,512]{1,0:T(1,128)} %bitcast.2, s32[1,512]{1,0:T(1,128)} %bitcast.3, f32[512,512]{1,0:T(8,128)} %grads_hbm.1, f32[2048,512]{1,0:T(8,128)} %table_hbm.1, ...), custom_call_target="tpu_custom_call" | custom-call | tf_op jit(solution)/shard_map/exchange/pallas_call | solution.py:242
  44.4 4.8 %update.1 = (f32[2048,512]{1,0:T(8,128)}, f32[2048,512]{1,0:T(8,128)}, f32[2048,512]{1,0:T(8,128)}) custom-call(f32[2,2048,256]{2,1,0:T(8,128)S(1)} %get-tuple-element.8.dense, f32[2048,512]{1,0:T(8,128)S(1)} %get-tuple-element.9.table, f32[2048,512]{1,0:T(8,128)S(1)} %get-tuple-element.10.moment, f32[2048,512]{1,0:T(8,128)S(1)} %get-tuple-element.11.second, ...), custom_call_target="tpu_custom_call" | custom-call | tf_op jit(solution)/shard_map/update/pallas_call | solution.py:332

commit v4 on v3

--- a/solution.py
+++ b/solution.py
@@ -145,20 +145,24 @@
 
     pl.semaphore_wait(barrier, 127)
 
+    def send_rows(first, last):
+        for j in range(first, last):
+            target = ahead(FAR_FIRST[j])
+            for flip in range(2):
+                half = (core + flip) % 2
+                pltpu.make_async_remote_copy(
+                    send.at[target, half], recv.at[(j // 8) * 16 + j % 8 + 8 * flip], send_sem,
+                    recv_sem.at[j // 8], device_id=(target, half), device_id_type=MESH,
+                ).start()
+
+    send_rows(0, 8)
     for j, offset in enumerate(FAR_FIRST):
         target = ahead(offset)
         pltpu.make_async_remote_copy(
             ids_send.at[target], ids_recv.at[j], ids_sem, ids_got,
             device_id=(target, core), device_id_type=MESH,
         ).start()
-    for j, offset in enumerate(FAR_FIRST):
-        target = ahead(offset)
-        for flip in range(2):
-            half = (core + flip) % 2
-            pltpu.make_async_remote_copy(
-                send.at[target, half], recv.at[(j // 8) * 16 + j % 8 + 8 * flip], send_sem,
-                recv_sem.at[j // 8], device_id=(target, half), device_id_type=MESH,
-            ).start()
+    send_rows(8, 63)
     pltpu.make_async_remote_copy(
         send.at[me, 1 - core], recv.at[127], send_sem, recv_sem.at[7],
         device_id=(me, 1 - core), device_id_type=MESH,

time: 49.3 us -> 49.3 us (level)
  no operation moved by 1% of the time
where the time goes in v4:
time: 49.3 us; the launch traced here: 49.2 us
  Pallas kernels  48.6 us (99%)
  between operations  0.64 us (1%)
    pallas_call x1, Pallas kernels, exchange(): pl.pallas_call(exchange_kernel, out_shape=(pltpu.VMEM((2, ROWS, HALF), F3...  43.8 us
    pallas_call x1, Pallas kernels, update(): pl.pallas_call(update_kernel, out_shape=(out, out, out), in_specs=[vmem]...  4.78 us

profile of v4, /device:TPU:1, one launch (start us, length us, event | category | flops | bytes accessed | tf_op | source)
XLA Modules:
  0.0 49.2 jit_solution(16905284109839040156)
XLA Ops:
  0.6 43.8 %exchange.1 = (f32[2,2048,256]{2,1,0:T(8,128)S(1)}, f32[2048,512]{1,0:T(8,128)S(1)}, f32[2048,512]{1,0:T(8,128)S(1)}, f32[2048,512]{1,0:T(8,128)S(1)}, f32[8,128]{1,0:T(8,128)S(1)}) custom-call(s32[1,512]{1,0:T(1,128)} %bitcast.2, s32[1,512]{1,0:T(1,128)} %bitcast.3, f32[512,512]{1,0:T(8,128)} %grads_hbm.1, f32[2048,512]{1,0:T(8,128)} %table_hbm.1, ...), custom_call_target="tpu_custom_call" | custom-call | tf_op jit(solution)/shard_map/exchange/pallas_call | solution.py:246
  44.4 4.8 %update.1 = (f32[2048,512]{1,0:T(8,128)}, f32[2048,512]{1,0:T(8,128)}, f32[2048,512]{1,0:T(8,128)}) custom-call(f32[2,2048,256]{2,1,0:T(8,128)S(1)} %get-tuple-element.8.dense, f32[2048,512]{1,0:T(8,128)S(1)} %get-tuple-element.9.table, f32[2048,512]{1,0:T(8,128)S(1)} %get-tuple-element.10.moment, f32[2048,512]{1,0:T(8,128)S(1)} %get-tuple-element.11.second, ...), custom_call_target="tpu_custom_call" | custom-call | tf_op jit(solution)/shard_map/update/pallas_call | solution.py:336
